TPU v7x, 32 devices: a whole 2x2x4 slice. The times are simulated.
32 devices in a mesh: row: 4 (over y, x), col: 4 (over z), rep: 2 (over core).
Axes of the slice: x: 2, y: 2, z: 4, core: 2. Of those that a mesh axis runs over, the one named last changes fastest.
Arguments:
- sources: int32 [64], replicated, may hold values from 0 to 4095
- tile_weights: int32 [1024, 128, 128], P(('row', 'col', 'rep')), may hold values from 0 to 16, as said below
- tile_src: int32 [1024], P(('row', 'col', 'rep')), may hold values from 0 to 31, as said below
- tile_dst: int32 [1024], P(('row', 'col', 'rep')), may hold values from 0 to 31, as said below
- tile_count: int32 [32], P(('row', 'col', 'rep')), may hold values from 1 to 32, 512 in all
Outputs:
- distances: float32 [64, 4096], P(None, ('row', 'col', 'rep'))
- recip_sums: float32 [16, 64], P(('row', 'col'))
Inputs may be any that keep to these rules, and one draw needn't show every extreme that they name: `tile_weights`: an entry of 0 means no edge; others are the edge's weight. `tile_src`: piece p = b // 1 of block b belongs to the device at mesh coordinates (row, col, rep) = (p // 8, (p // 2) % 4, p % 2); slot k belongs to device k // 32 in the same numbering. A tile's source block lies in a piece whose col index is that of the tile's device. `tile_dst`: A tile's destination block lies in a piece whose row and rep indices are those of the tile's device, in the numbering given for tile_src. Only the first tile_count[d] slots of device d hold live tiles; some device has all 32 slots live.
All inputs are finite; a program needn't handle non-finite values.
Results may differ from a plain program's by a relative error of at most 0.0003.
Values may be sent and summed in bfloat16 or wider, within the bound.
No kernel may reach another device: no remote copies, remote signals or barrier semaphores. Data moves between devices by JAX's collectives and lax.ppermute only.
A program may use at most 64 MiB of HBM per device.

v0:
```python
import jax
import jax.numpy as jnp
from jax import lax
from jax.sharding import PartitionSpec as P

BLK_DEV = 1
TILE_DEV = 32
BS = 128
ROUNDS = 2
far_value = 255.0


def relax_tiles(gathered, weights, src_pos, dst_pos, ordering, live_total, blocks_out):
    height = gathered.shape[0]
    partial_value = jnp.full((height, blocks_out * BS), far_value, jnp.bfloat16)

    def relax_four(step_no, partial_value):
        for offset in range(4):
            slot_now = 4 * step_no + offset
            picked = ordering[slot_now]
            weight = lax.dynamic_index_in_dim(weights, picked, 0, keepdims=False)
            source = lax.dynamic_slice_in_dim(gathered, src_pos[picked] * BS, BS, 1)
            candidate = jnp.min(source[:, :, None] + weight[None, :, :], axis=1)
            candidate = jnp.where(slot_now < live_total, candidate, jnp.bfloat16(far_value))
            begin_at = dst_pos[picked] * BS
            previous = lax.dynamic_slice_in_dim(partial_value, begin_at, BS, 1)
            partial_value = lax.dynamic_update_slice_in_dim(
                partial_value, jnp.minimum(previous, candidate), begin_at, 1
            )
        return partial_value

    return lax.fori_loop(0, (live_total + 3) // 4, relax_four, partial_value)


def source_slot(block_ids, n_col, n_rep):
    piece_id = block_ids // BLK_DEV
    return (piece_id // (n_col * n_rep) * n_rep + piece_id % n_rep) * BLK_DEV + block_ids % BLK_DEV


def per_device(sources, tile_weights, tile_src, tile_dst, tile_count):
    n_col = lax.axis_size("col")
    n_rep = lax.axis_size("rep")
    width = BLK_DEV * BS
    sources_all = sources.shape[0]
    piece_id = (lax.axis_index("row") * n_col + lax.axis_index("col")) * n_rep + lax.axis_index(
        "rep"
    )
    columns = piece_id * width + jnp.arange(width, dtype=jnp.int32)
    dist = jnp.where(columns[None, :] == sources[:, None], 0.0, far_value).astype(jnp.bfloat16)
    weights = jnp.where(tile_weights > 0, tile_weights.astype(jnp.float32), far_value).astype(
        jnp.bfloat16
    )
    ordering = jnp.arange(TILE_DEV, dtype=jnp.int32)
    live_total = tile_count[0]
    src_pos = source_slot(tile_src, n_col, n_rep)
    dest_piece = tile_dst // BLK_DEV
    dst_pos = dest_piece // n_rep % n_col * BLK_DEV + tile_dst % BLK_DEV
    for round_no in range(ROUNDS):
        gathered = lax.all_gather(dist, ("row", "rep"), axis=1, tiled=True)
        partial_value = relax_tiles(
            gathered, weights, src_pos, dst_pos, ordering, live_total, n_col * BLK_DEV
        )
        fresh = jnp.min(
            lax.all_to_all(
                partial_value.reshape(sources_all, 1, n_col * width),
                "col",
                split_axis=2,
                concat_axis=1,
                tiled=True,
            ),
            axis=1,
        )
        dist = jnp.minimum(dist, fresh)
    as_float = dist.astype(jnp.float32)
    inverse = jnp.where(as_float > 0, 1.0 / jnp.maximum(as_float, 1.0), 0.0)
    sums = lax.psum(jnp.sum(inverse, axis=1), "rep")
    return (as_float, sums[None, :])


def solution(mesh):
    return jax.shard_map(
        per_device,
        mesh=mesh,
        in_specs=(
            P(),
            P(("row", "col", "rep"), None, None),
            P(("row", "col", "rep")),
            P(("row", "col", "rep")),
            P(("row", "col", "rep")),
        ),
        out_specs=(P(None, ("row", "col", "rep")), P(("row", "col"), None)),
        check_vma=False,
    )
```

profile of v0, /device:TPU:0, one launch (start us, length us, event | category | flops | bytes accessed | tf_op | source)
XLA Modules:
  0.0 407.2 jit_solution(2897030421059010277)
XLA Ops:
  2.1 10.5 %all_gather.6 = bf16[64,1024]{1,0:T(8,128)(2,1)S(1)} all-gather(bf16[64,128]{1,0:T(8,128)(2,1)S(1)} %select_convert_fusion.1), channel_id=1, replica_groups=mesh['row'=4,'col'=4,'rep'=2] {'row','rep'}, dimensions={1}, use_global_device_ids=true | all-gather | bytes 147456 | tf_op jit(solution)/shard_map/all_gather | solution.py:59
  12.6 2.6 select_convert_fusion
  15.3 178.3 %while.26 = (s32[]{:T(128)}, bf16[64,512]{1,0:T(8,128)(2,1)S(1)}, s32[]{:T(128)}, s32[32]{0:T(128)S(1)}, s32[32]{0:T(128)S(1)}, /*index=5*/s32[]{:T(128)}, s32[3...) while((s32[]{:T(128)}, bf16[64,512]{1,0:T(8,128)(2,1)S(1)}, ...), condition=%wide.region_5.6_spmd.clone, body=%wide.region_0.5_spmd.clone.sunk | while | flops 8519746 | bytes 853061 | solution.py:32
  26.9 1.4 add_reduce_fusion.18
  28.2 1.4 add_reduce_fusion.17
  29.6 1.4 add_reduce_fusion.16
  34.9 1.4 add_reduce_fusion.19
  49.2 1.4 add_reduce_fusion.18
  50.5 1.4 add_reduce_fusion.17
  51.9 1.4 add_reduce_fusion.16
  57.1 1.4 add_reduce_fusion.19
  71.4 1.4 add_reduce_fusion.18
  72.8 1.4 add_reduce_fusion.17
  74.2 1.4 add_reduce_fusion.16
  79.4 1.4 add_reduce_fusion.19
  93.7 1.4 add_reduce_fusion.18
  95.1 1.4 add_reduce_fusion.17
  96.5 1.4 add_reduce_fusion.16
  101.7 1.4 add_reduce_fusion.19
  116.0 1.4 add_reduce_fusion.18
  117.4 1.4 add_reduce_fusion.17
  118.8 1.4 add_reduce_fusion.16
  124.0 1.4 add_reduce_fusion.19
  138.3 1.4 add_reduce_fusion.18
  139.7 1.4 add_reduce_fusion.17
  141.1 1.4 add_reduce_fusion.16
  146.3 1.4 add_reduce_fusion.19
  160.6 1.4 add_reduce_fusion.18
  162.0 1.4 add_reduce_fusion.17
  168.6 1.4 add_reduce_fusion.19
  182.9 1.4 add_reduce_fusion.18
  184.3 1.4 add_reduce_fusion.17
  185.6 1.4 add_reduce_fusion.16
  190.9 1.4 add_reduce_fusion.19
  194.3 1.4 reduce.4
  196.5 4.9 %all-to-all-start = ((bf16[4,2,4096]{2,1,0:T(2,128)(2,1)}), bf16[4,2,4096]{2,1,0:T(2,128)(2,1)S(1)}, u32[]{:S(2)}, u32[]{:S(2)}) async-start(bf16[4,2,4096]{2,1,0:T(2,128)(2,1)} %reshape.63), calls=%async_computation | async-start | bytes 131072 | tf_op jit(solution)/shard_map/all_to_all | solution.py:64
  201.4 5.7 %all-to-all-done = bf16[4,2,4096]{2,1,0:T(2,128)(2,1)S(1)} async-done(((bf16[4,2,4096]{2,1,0:T(2,128)(2,1)}), bf16[4,2,4096]{2,1,0:T(2,128)(2,1)S(1)}, u32[]{:S(2)}, u32[]{:S(2)}) %all-to-all-start) | async-done | bytes 65568 | tf_op jit(solution)/shard_map/all_to_all | solution.py:64
  207.6 7.6 %all_gather.7 = bf16[64,1024]{1,0:T(8,128)(2,1)S(1)} all-gather(bf16[64,128]{1,0:T(8,128)(2,1)S(1)} %fusion), channel_id=1, replica_groups=mesh['row'=4,'col'=4,'rep'=2] {'row','rep'}, dimensions={1}, use_global_device_ids=true | all-gather | bytes 147456 | tf_op jit(solution)/shard_map/all_gather | solution.py:59
  215.2 177.9 %while.27 = (s32[]{:T(128)}, bf16[64,512]{1,0:T(8,128)(2,1)S(1)}, s32[]{:T(128)}, s32[32]{0:T(128)S(1)}, s32[32]{0:T(128)S(1)}, /*index=5*/s32[]{:T(128)}, s32[3...) while((s32[]{:T(128)}, bf16[64,512]{1,0:T(8,128)(2,1)S(1)}, ...), condition=%wide.region_12.13_spmd.clone, body=%wide.region_7.12_spmd.clone.sunk | while | flops 8519746 | bytes 853061 | solution.py:32
  226.7 1.4 add_reduce_fusion.22
  228.1 1.4 add_reduce_fusion.21
  234.7 1.4 add_reduce_fusion.23
  250.4 1.4 add_reduce_fusion.21
  257.0 1.4 add_reduce_fusion.23
  272.6 1.4 add_reduce_fusion.21
  279.2 1.4 add_reduce_fusion.23
  293.5 1.4 add_reduce_fusion.22
  294.8 1.4 add_reduce_fusion.21
  296.2 1.4 add_reduce_fusion.20
  301.4 1.4 add_reduce_fusion.23
  315.7 1.4 add_reduce_fusion.22
  317.1 1.4 add_reduce_fusion.21
  318.4 1.4 add_reduce_fusion.20
  337.9 1.4 add_reduce_fusion.22
  340.7 1.4 add_reduce_fusion.20
  360.2 1.4 add_reduce_fusion.22
  362.9 1.4 add_reduce_fusion.20
  368.2 1.4 add_reduce_fusion.23
  382.4 1.4 add_reduce_fusion.22
  385.1 1.4 add_reduce_fusion.20
  390.4 1.4 add_reduce_fusion.23
  393.3 1.4 reduce.5
  394.9 8.1 %all_to_all.24 = bf16[4,2,4096]{2,1,0:T(2,128)(2,1)S(1)} all-to-all(bf16[4,2,4096]{2,1,0:T(2,128)(2,1)S(1)} %reshape.65), channel_id=1, replica_groups=mesh['row'=4,'col'=4,'rep'=2] {'col'}, dimensions={0} | all-to-all | bytes 131072 | tf_op jit(solution)/shard_map/all_to_all | solution.py:64
  404.2 3.0 psum.7
  (167 shorter events, 43.6 us)
Async XLA Ops:
  0.6 14.6 %copy-start.2 = (s32[32]{0:T(128)S(1)}, s32[32]{0:T(128)}, u32[]{:S(2)}) copy-start(s32[32]{0:T(128)} %param.11) | copy-start | bytes 388
  0.6 14.6 %copy-start.1 = (s32[32]{0:T(128)S(1)}, s32[32]{0:T(128)}, u32[]{:S(2)}) copy-start(s32[32]{0:T(128)} %param.12) | copy-start | bytes 388
  15.3 192.2 %copy-start = (s32[64]{0:T(128)S(1)}, s32[64]{0:T(128)}, u32[]{:S(2)}) copy-start(s32[64]{0:T(128)} %param.9) | copy-start | bytes 772
  196.5 10.6 %all-to-all-start = ((bf16[4,2,4096]{2,1,0:T(2,128)(2,1)}), bf16[4,2,4096]{2,1,0:T(2,128)(2,1)S(1)}, u32[]{:S(2)}, u32[]{:S(2)}) async-start(bf16[4,2,4096]{2,1,0:T(2,128)(2,1)} %reshape.63), calls=%async_computation | async-start | bytes 131072 | tf_op jit(solution)/shard_map/all_to_all | solution.py:64
where the time goes:
time: 411 us; the launch traced here: 407 us
  loops' own time  244 us (59%)
  other arithmetic  96 us (23%)
  blocking collectives  29.2 us (7%)
  local copies, waits for them, and re-layouts  25.5 us (6%)
  waiting for transfers between devices  5.74 us (1%)
  starting transfers between devices  4.87 us (1%)
    another operation x2, loops' own time, relax_tiles(): return lax.fori_loop(0, (live_total + 3) // 4, relax_four, partial_value)  244 us
    reduce_min x64, other arithmetic, relax_four(): candidate = jnp.min(source[:, :, None] + weight[None, :, :], axis=1)  87.5 us
    all_gather x2, blocking collectives, per_device(): gathered = lax.all_gather(dist, ('row', 'rep'), axis=1, tiled=True)  18.1 us
    dynamic_slice x32, local copies, waits for them, and re-layouts, relax_four(): source = lax.dynamic_slice_in_dim(gathered, src_pos[picked] * BS, BS, 1)  11.8 us
    dynamic_slice x16, local copies, waits for them, and re-layouts, relax_four(): picked = ordering[slot_now]  11 us
  transfers between devices with their start and end apart: 1, of which 1 were waited for; matrix products, arithmetic and copies ran while one was open for 0% of the time, Pallas kernels for 0%

commit v1 on v0

--- a/solution.py
+++ b/solution.py
@@ -2,12 +2,34 @@
 import jax.numpy as jnp
 from jax import lax
 from jax.sharding import PartitionSpec as P
+from jax.lax import axis_index, ppermute, psum
 
 BLK_DEV = 1
 TILE_DEV = 32
 BS = 128
 ROUNDS = 2
 far_value = 255.0
+
+
+def move_pipes(incoming_x):
+    opened = psum(1, axis_name="col")
+    arr_next = axis_index("col")
+    x_now, lower = (opened, arr_next)
+    base_arr = list(incoming_x.shape)
+    passed = incoming_x.shape[2] // x_now
+    base_arr[2] = passed
+    parts_out = base_arr[1]
+    base_arr[1] = parts_out * x_now
+    oldest = jnp.zeros(base_arr, incoming_x.dtype)
+    for c in range(x_now):
+        z2 = lax.dynamic_slice_in_dim(incoming_x, (lower ^ c) * passed, passed, axis=2)
+        if c:
+            kept_arr = range(x_now)
+            tmp = map(lambda j: (j, j ^ c), kept_arr)
+            top = list(tmp)
+            z2 = ppermute(z2, axis_name="col", perm=top)
+        oldest = lax.dynamic_update_slice_in_dim(oldest, z2, (lower ^ c) * parts_out, axis=1)
+    return oldest
 
 
 def relax_tiles(gathered, weights, src_pos, dst_pos, ordering, live_total, blocks_out):
@@ -60,16 +82,7 @@
         partial_value = relax_tiles(
             gathered, weights, src_pos, dst_pos, ordering, live_total, n_col * BLK_DEV
         )
-        fresh = jnp.min(
-            lax.all_to_all(
-                partial_value.reshape(sources_all, 1, n_col * width),
-                "col",
-                split_axis=2,
-                concat_axis=1,
-                tiled=True,
-            ),
-            axis=1,
-        )
+        fresh = jnp.min(move_pipes(partial_value.reshape(sources_all, 1, n_col * width)), axis=1)
         dist = jnp.minimum(dist, fresh)
     as_float = dist.astype(jnp.float32)
     inverse = jnp.where(as_float > 0, 1.0 / jnp.maximum(as_float, 1.0), 0.0)

time: 411 us -> 404 us (0.983)
  blocking collectives: 29.2 us -> 21.1 us
    ppermute x0 -> x6, starting transfers between devices: none -> 8.95 us  [move_pipes(): z2 = ppermute(z2, axis_name='col', perm=top)]
    ppermute x0 -> x6, waiting for transfers between devices: none -> 8.22 us  [move_pipes(): z2 = ppermute(z2, axis_name='col', perm=top)]
    all_to_all x1 -> x0, blocking collectives: 8.11 us -> none  [per_device(): lax.all_to_all(partial_value.reshape(sources_all, 1, n_col * width), 'col...]
    all_to_all x1 -> x0, waiting for transfers between devices: 5.74 us -> none  [per_device(): lax.all_to_all(partial_value.reshape(sources_all, 1, n_col * width), 'col...]
    all_to_all x1 -> x0, starting transfers between devices: 4.87 us -> none  [per_device(): lax.all_to_all(partial_value.reshape(sources_all, 1, n_col * width), 'col...]
  transfers between devices with their start and end apart: 1 -> 6, of which waited for: 1 -> 4; matrix products, arithmetic and copies ran while one was open for 0% -> 0% of each run, Pallas kernels for 0% -> 0%
where the time goes in v1:
time: 404 us; the launch traced here: 401 us
  loops' own time  245 us (61%)
  other arithmetic  93.1 us (23%)
  local copies, waits for them, and re-layouts  23.3 us (6%)
  blocking collectives  21.1 us (5%)
  starting transfers between devices  8.95 us (2%)
  waiting for transfers between devices  8.22 us (2%)
    another operation x2, loops' own time, relax_tiles(): return lax.fori_loop(0, (live_total + 3) // 4, relax_four, partial_value)  245 us
    reduce_min x64, other arithmetic, relax_four(): candidate = jnp.min(source[:, :, None] + weight[None, :, :], axis=1)  87.5 us
    all_gather x2, blocking collectives, per_device(): gathered = lax.all_gather(dist, ('row', 'rep'), axis=1, tiled=True)  18.1 us
    dynamic_slice x32, local copies, waits for them, and re-layouts, relax_four(): source = lax.dynamic_slice_in_dim(gathered, src_pos[picked] * BS, BS, 1)  11.8 us
    dynamic_slice x16, local copies, waits for them, and re-layouts, relax_four(): picked = ordering[slot_now]  11 us
    ppermute x6, starting transfers between devices, move_pipes(): z2 = ppermute(z2, axis_name='col', perm=top)  8.95 us
    ppermute x6, waiting for transfers between devices, move_pipes(): z2 = ppermute(z2, axis_name='col', perm=top)  8.22 us
  transfers between devices with their start and end apart: 6, of which 4 were waited for; matrix products, arithmetic and copies ran while one was open for 0% of the time, Pallas kernels for 0%

profile of v1, /device:TPU:0, one launch (start us, length us, event | category | flops | bytes accessed | tf_op | source)
XLA Modules:
  0.0 400.9 jit_solution(3491207965316013446)
XLA Ops:
  2.1 10.5 %all_gather.6 = bf16[64,1024]{1,0:T(8,128)(2,1)S(1)} all-gather(bf16[64,128]{1,0:T(8,128)(2,1)S(1)} %select_convert_fusion.1), channel_id=1, replica_groups=mesh['row'=4,'col'=4,'rep'=2] {'row','rep'}, dimensions={1}, use_global_device_ids=true | all-gather | bytes 147456 | tf_op jit(solution)/shard_map/all_gather | solution.py:81
  12.6 2.6 select_convert_fusion
  15.3 178.3 %while.26 = (s32[]{:T(128)}, bf16[64,512]{1,0:T(8,128)(2,1)S(1)}, s32[]{:T(128)}, s32[32]{0:T(128)S(1)}, s32[32]{0:T(128)S(1)}, /*index=5*/s32[]{:T(128)}, s32[3...) while((s32[]{:T(128)}, bf16[64,512]{1,0:T(8,128)(2,1)S(1)}, ...), condition=%wide.region_5.6_spmd.clone, body=%wide.region_0.5_spmd.clone.sunk | while | flops 8519746 | bytes 853061 | solution.py:54
  26.9 1.4 add_reduce_fusion.18
  28.3 1.4 add_reduce_fusion.17
  29.6 1.4 add_reduce_fusion.16
  34.9 1.4 add_reduce_fusion.19
  49.2 1.4 add_reduce_fusion.18
  50.5 1.4 add_reduce_fusion.17
  51.9 1.4 add_reduce_fusion.16
  57.2 1.4 add_reduce_fusion.19
  71.5 1.4 add_reduce_fusion.18
  72.8 1.4 add_reduce_fusion.17
  74.2 1.4 add_reduce_fusion.16
  79.4 1.4 add_reduce_fusion.19
  93.7 1.4 add_reduce_fusion.18
  95.1 1.4 add_reduce_fusion.17
  96.5 1.4 add_reduce_fusion.16
  101.7 1.4 add_reduce_fusion.19
  116.0 1.4 add_reduce_fusion.18
  117.4 1.4 add_reduce_fusion.17
  118.8 1.4 add_reduce_fusion.16
  124.0 1.4 add_reduce_fusion.19
  139.7 1.4 add_reduce_fusion.17
  146.3 1.4 add_reduce_fusion.19
  162.0 1.4 add_reduce_fusion.17
  168.6 1.4 add_reduce_fusion.19
  182.9 1.4 add_reduce_fusion.18
  184.3 1.4 add_reduce_fusion.17
  185.6 1.4 add_reduce_fusion.16
  190.9 1.4 add_reduce_fusion.19
  193.8 4.2 %collective-permute-start.1 = (bf16[64,1,128]{2,0,1:T(8,128)(2,1)S(1)}, bf16[64,1,128]{2,0,1:T(8,128)(2,1)S(1)}, u32[]{:S(2)}, u32[]{:S(2)}) collective-permute-start(bf16[64,1,128]{2,0,1:T(8,128)(2,1)S(1)} %get-tuple-element.398), channel_id=1, source_target_pairs={{0,4},{2,6},{4,0},{6,2},{1,5},{3,7},{5,1},{7,3},{8,12},{10,14},{12... | collective-permute-start | bytes 49160 | tf_op jit(solution)/shard_map/ppermute | solution.py:30
  198.2 1.4 collective-permute-done.1
  199.6 3.8 collective-permute-done.2
  203.6 7.6 %all_gather.7 = bf16[64,1024]{1,0:T(8,128)(2,1)S(1)} all-gather(bf16[64,128]{1,0:T(8,128)(2,1)S(1)} %fusion), channel_id=1, replica_groups=mesh['row'=4,'col'=4,'rep'=2] {'row','rep'}, dimensions={1}, use_global_device_ids=true | all-gather | bytes 147456 | tf_op jit(solution)/shard_map/all_gather | solution.py:81
  211.2 178.3 %while.27 = (s32[]{:T(128)}, bf16[64,512]{1,0:T(8,128)(2,1)S(1)}, s32[]{:T(128)}, s32[32]{0:T(128)S(1)}, s32[32]{0:T(128)S(1)}, /*index=5*/s32[]{:T(128)}, s32[3...) while((s32[]{:T(128)}, bf16[64,512]{1,0:T(8,128)(2,1)S(1)}, ...), condition=%wide.region_12.13_spmd.clone, body=%wide.region_7.12_spmd.clone.sunk | while | flops 8519746 | bytes 853061 | solution.py:54
  222.7 1.4 add_reduce_fusion.22
  225.5 1.4 add_reduce_fusion.20
  230.7 1.4 add_reduce_fusion.23
  245.0 1.4 add_reduce_fusion.22
  246.4 1.4 add_reduce_fusion.21
  247.8 1.4 add_reduce_fusion.20
  253.0 1.4 add_reduce_fusion.23
  268.7 1.4 add_reduce_fusion.21
  275.3 1.4 add_reduce_fusion.23
  289.6 1.4 add_reduce_fusion.22
  291.0 1.4 add_reduce_fusion.21
  292.3 1.4 add_reduce_fusion.20
  311.9 1.4 add_reduce_fusion.22
  314.6 1.4 add_reduce_fusion.20
  319.9 1.4 add_reduce_fusion.23
  334.2 1.4 add_reduce_fusion.22
  335.5 1.4 add_reduce_fusion.21
  336.9 1.4 add_reduce_fusion.20
  342.1 1.4 add_reduce_fusion.23
  357.8 1.4 add_reduce_fusion.21
  364.4 1.4 add_reduce_fusion.23
  378.7 1.4 add_reduce_fusion.22
  380.1 1.4 add_reduce_fusion.21
  381.5 1.4 add_reduce_fusion.20
  389.6 1.9 collective-permute-start.4
  391.5 2.5 collective-permute-start.5
  394.3 2.7 collective-permute-done.5
  397.9 3.0 psum.7
  (175 shorter events, 43.3 us)
Async XLA Ops:
  0.6 14.6 %copy-start.2 = (s32[32]{0:T(128)S(1)}, s32[32]{0:T(128)}, u32[]{:S(2)}) copy-start(s32[32]{0:T(128)} %param.11) | copy-start | bytes 388
  0.6 14.6 %copy-start.1 = (s32[32]{0:T(128)S(1)}, s32[32]{0:T(128)}, u32[]{:S(2)}) copy-start(s32[32]{0:T(128)} %param.12) | copy-start | bytes 388
  15.3 188.2 %copy-start = (s32[64]{0:T(128)S(1)}, s32[64]{0:T(128)}, u32[]{:S(2)}) copy-start(s32[64]{0:T(128)} %param.9) | copy-start | bytes 772
  193.7 4.5 %collective-permute-start = (bf16[64,1,128]{2,0,1:T(8,128)(2,1)S(1)}, bf16[64,1,128]{2,0,1:T(8,128)(2,1)S(1)}, u32[]{:S(2)}, u32[]{:S(2)}) collective-permute-start(bf16[64,1,128]{2,0,1:T(8,128)(2,1)S(1)} %get-tuple-element.399), channel_id=1, source_target_pairs={{0,2},{2,0},{4,6},{6,4},{1,3},{3,1},{5,7},{7,5},{8,10},{10,8},{12,... | collective-permute-start | bytes 49160 | tf_op jit(solution)/shard_map/ppermute | solution.py:30
  193.8 5.9 %collective-permute-start.1 = (bf16[64,1,128]{2,0,1:T(8,128)(2,1)S(1)}, bf16[64,1,128]{2,0,1:T(8,128)(2,1)S(1)}, u32[]{:S(2)}, u32[]{:S(2)}) collective-permute-start(bf16[64,1,128]{2,0,1:T(8,128)(2,1)S(1)} %get-tuple-element.398), channel_id=1, source_target_pairs={{0,4},{2,6},{4,0},{6,2},{1,5},{3,7},{5,1},{7,3},{8,12},{10,14},{12... | collective-permute-start | bytes 49160 | tf_op jit(solution)/shard_map/ppermute | solution.py:30
  197.9 5.5 %collective-permute-start.2 = (bf16[64,1,128]{2,0,1:T(8,128)(2,1)S(1)}, bf16[64,1,128]{2,0,1:T(8,128)(2,1)S(1)}, u32[]{:S(2)}, u32[]{:S(2)}) collective-permute-start(bf16[64,1,128]{2,0,1:T(8,128)(2,1)S(1)} %get-tuple-element.397), channel_id=1, source_target_pairs={{0,6},{2,4},{4,2},{6,0},{1,7},{3,5},{5,3},{7,1},{8,14},{10,12},{12... | collective-permute-start | bytes 49160 | tf_op jit(solution)/shard_map/ppermute | solution.py:30
  389.5 4.6 %collective-permute-start.3 = (bf16[64,1,128]{2,0,1:T(8,128)(2,1)S(1)}, bf16[64,1,128]{2,0,1:T(8,128)(2,1)S(1)}, u32[]{:S(2)}, u32[]{:S(2)}) collective-permute-start(bf16[64,1,128]{2,0,1:T(8,128)(2,1)S(1)} %get-tuple-element.396), channel_id=1, source_target_pairs={{0,2},{2,0},{4,6},{6,4},{1,3},{3,1},{5,7},{7,5},{8,10},{10,8},{12,... | collective-permute-start | bytes 49160 | tf_op jit(solution)/shard_map/ppermute | solution.py:30
  389.6 4.7 %collective-permute-start.4 = (bf16[64,1,128]{2,0,1:T(8,128)(2,1)S(1)}, bf16[64,1,128]{2,0,1:T(8,128)(2,1)S(1)}, u32[]{:S(2)}, u32[]{:S(2)}) collective-permute-start(bf16[64,1,128]{2,0,1:T(8,128)(2,1)S(1)} %get-tuple-element.395), channel_id=1, source_target_pairs={{0,4},{2,6},{4,0},{6,2},{1,5},{3,7},{5,1},{7,3},{8,12},{10,14},{12... | collective-permute-start | bytes 49160 | tf_op jit(solution)/shard_map/ppermute | solution.py:30
  391.5 5.5 %collective-permute-start.5 = (bf16[64,1,128]{2,0,1:T(8,128)(2,1)S(1)}, bf16[64,1,128]{2,0,1:T(8,128)(2,1)S(1)}, u32[]{:S(2)}, u32[]{:S(2)}) collective-permute-start(bf16[64,1,128]{2,0,1:T(8,128)(2,1)S(1)} %get-tuple-element.394), channel_id=1, source_target_pairs={{0,6},{2,4},{4,2},{6,0},{1,7},{3,5},{5,3},{7,1},{8,14},{10,12},{12... | collective-permute-start | bytes 49160 | tf_op jit(solution)/shard_map/ppermute | solution.py:30
